TPU v7x, 32 devices: a whole 2x2x4 slice. The times are simulated.
32 devices in a mesh: cls: 4 (over y, x), org: 8 (over z, core).
Axes of the slice: x: 2, y: 2, z: 4, core: 2. Of those that a mesh axis runs over, the one named last changes fastest.
Arguments:
- flows_start: float32 [8, 49152], P('cls', 'org'), may hold values from 150 to 300
- interaction: float32 [8, 8, 49152], P('cls', None, 'org'), may hold values from 0.2 to 2
- free_time: float32 [8, 49152], P('cls', 'org'), may hold values from 0.01 to 0.1
- capacity: float32 [49152], P('org'), may hold values from 300 to 900
- demand: int32 [8, 8, 60], P('cls', 'org'), may hold values from 0 to 15
- incidence: int32 [2, 8, 8, 2, 49152], P(None, 'cls', 'org'), may hold values from 0 to 1073741823, as said below
- step_size: float32 [2], replicated, may hold values from 0.3 to 0.6
Outputs:
- flows: float32 [8, 49152], P('cls', 'org')
- costs: float32 [8, 49152], P('cls', 'org')
- skims: float32 [2, 8, 8, 60], P(None, 'cls', 'org')
- gaps: float32 [2], replicated
Inputs may be any that keep to these rules, and one draw needn't show every extreme that they name: Bit b of incidence[k, c, o, w, l] tells whether link l lies on class c's path from anchor o to destination w * 30 + b in iteration k; each path is the union of 4 runs of 64 consecutive links (counted cyclically over the links) at drawn starts, the first of which is shared by all 30 destinations of one word.
All inputs are finite; a program needn't handle non-finite values.
Results may differ from a plain program's by a relative error of at most 0.0013.
Values sent between devices are 32-bit elements; how exact they have to be, the bound alone decides.
A program may use at most 256 MiB of HBM per device.

v0:
```python
import jax
import jax.numpy as jnp
from jax import lax
from jax.sharding import PartitionSpec as P

BITS = 30
ITERS = 2
HIGH = lax.Precision.HIGHEST


def unpack_half(packed):
    shifts = jnp.arange(BITS, dtype=jnp.int32)
    bit_table = jnp.bitwise_and(jnp.right_shift(packed[..., :, None, :], shifts[:, None]), 1)
    new_shape = packed.shape[:-2] + (packed.shape[-2] * BITS, packed.shape[-1])
    return bit_table.reshape(new_shape).astype(jnp.bfloat16)


def link_cost(flows_all, inter, free, cap):
    load_sum = jnp.einsum("cel,el->cl", inter, flows_all, precision=HIGH)
    load_ratio = load_sum / cap
    square = load_ratio * load_ratio
    return free * (1.0 + 0.15 * square * square)


def split_three(values):
    upper = values.astype(jnp.bfloat16)
    remain = values - upper.astype(jnp.float32)
    middle = remain.astype(jnp.bfloat16)
    lowest = (remain - middle.astype(jnp.float32)).astype(jnp.bfloat16)
    return jnp.stack([upper, middle, lowest], axis=1)


def skim_block(bit_table, cost_block):
    parts = split_three(cost_block)
    terms = jnp.einsum("codl,cpl->cpod", bit_table, parts, preferred_element_type=jnp.float32)
    return jnp.sum(terms, axis=1)


def anchor_loads_local(packed_all, trips_half, link_shard, block_count):

    def one_block(block_index):
        word_block = lax.dynamic_slice_in_dim(packed_all, block_index * link_shard, link_shard, 3)
        bit_table = unpack_half(word_block)
        return jnp.einsum("cod,codl->cl", trips_half, bit_table, preferred_element_type=jnp.float32)

    blocks = lax.map(one_block, jnp.arange(block_count, dtype=jnp.int32))
    return jnp.moveaxis(blocks, 0, 1).reshape(blocks.shape[1], block_count * link_shard)


def make_fold(packed_all, link_shard):

    def fold_links(skim_carry, portion, first):
        turn_count = portion.shape[1] // link_shard

        def advance(skim_sum, block_index):
            offset = block_index * link_shard
            word_block = lax.dynamic_slice_in_dim(packed_all, offset, link_shard, 3)
            bit_table = unpack_half(word_block)
            cost_block = lax.dynamic_slice_in_dim(portion, offset, link_shard, 1)
            return (skim_sum + skim_block(bit_table, cost_block), None)

        result, unused = lax.scan(advance, skim_carry, jnp.arange(turn_count, dtype=jnp.int32))
        return result

    return fold_links


def both_totals(cost_part, path_part):
    return lax.psum((cost_part, path_part), ("cls", "org"))


def shards(flows_start, interaction, free_time, capacity, demand, incidence, step_size):
    org_count = lax.axis_size("org")
    link_shard = flows_start.shape[1]
    dest_count = demand.shape[2]
    class_local = demand.shape[0]
    demand_real = demand.astype(jnp.float32)
    trips_half = demand.astype(jnp.bfloat16)
    own_start = lax.axis_index("org") * link_shard
    skim_init = jnp.zeros((class_local, demand.shape[1], dest_count), jnp.float32)
    skim_list = []
    gap_list = []
    inter_full, free_full, cap_full, flow_now = (
        lax.all_gather(interaction, "org", axis=2, tiled=True),
        lax.all_gather(free_time, "org", axis=1, tiled=True),
        lax.all_gather(capacity, "org", axis=0, tiled=True),
        lax.all_gather(flows_start, "org", axis=1, tiled=True),
    )

    def full_cost(flow_value):
        flows_all = lax.all_gather(flow_value, "cls", axis=0, tiled=True)
        return link_cost(flows_all, inter_full, free_full, cap_full)

    for iteration in range(ITERS):
        cost_now = full_cost(flow_now)
        fold_links = make_fold(incidence[iteration], link_shard)
        skim_now = fold_links(skim_init, cost_now, jnp.int32(0))
        partial_value = anchor_loads_local(incidence[iteration], trips_half, link_shard, org_count)
        aon = lax.psum(partial_value, "org")
        product = lax.dynamic_slice_in_dim(cost_now * flow_now, own_start, link_shard, 1)
        cost_total, path_total = both_totals(jnp.sum(product), jnp.sum(demand_real * skim_now))
        gap_list.append((cost_total - path_total) / cost_total)
        skim_list.append(skim_now)
        flow_now = flow_now + step_size[iteration] * (aon - flow_now)
    cost_final = full_cost(flow_now)
    flow_out = lax.dynamic_slice_in_dim(flow_now, own_start, link_shard, 1)
    cost_out = lax.dynamic_slice_in_dim(cost_final, own_start, link_shard, 1)
    return (flow_out, cost_out, jnp.stack(skim_list), jnp.stack(gap_list))


def solution(mesh):
    placed = (
        P("cls", "org"),
        P("cls", None, "org"),
        P("cls", "org"),
        P("org"),
        P("cls", "org", None),
        P(None, "cls", "org", None, None),
        P(),
    )
    return jax.shard_map(
        shards,
        mesh=mesh,
        in_specs=placed,
        out_specs=(P("cls", "org"), P("cls", "org"), P(None, "cls", "org", None), P()),
        check_vma=False,
    )
```

profile of v0, /device:TPU:0, one launch (start us, length us, event | category | flops | bytes accessed | tf_op | source)
XLA Modules:
  0.0 387.4 jit_solution(10713880894416797273)
XLA Ops:
  10.9 32.3 %while.43 = (s32[]{:T(128)}, f32[8,2,6144]{2,1,0:T(2,128)S(1)}, s32[8]{0:T(128)S(1)}, s32[2,1,2,49152]{3,0,2,1:T(2,128)S(1)}, bf16[2,1,60]{2,0,1:T(2,128)(2,1)S(...) while((s32[]{:T(128)}, f32[8,2,6144]{2,1,0:T(2,128)S(1)}, s32[8]{0:T(128)S(1)}, ...), condition=%wide.region_4.5_spmd, body=%wide.region_3.4_spmd.sunk | while | flops 3686406 | bytes 3392847 | solution.py:46
  12.3 1.7 fusion.83
  16.3 1.7 fusion.83
  28.4 1.7 fusion.83
  32.5 1.7 fusion.83
  36.5 1.7 fusion.83
  40.5 1.7 fusion.83
  44.3 32.3 %while.42 = (s32[]{:T(128)}, f32[8,2,6144]{2,1,0:T(2,128)S(1)}, s32[8]{0:T(128)S(1)}, s32[2,1,2,49152]{3,0,2,1:T(2,128)S(1)}, bf16[2,1,60]{2,0,1:T(2,128)(2,1)S(...) while((s32[]{:T(128)}, f32[8,2,6144]{2,1,0:T(2,128)S(1)}, s32[8]{0:T(128)S(1)}, ...), condition=%wide.region_1.0_spmd, body=%wide.region_0.1_spmd.sunk | while | flops 3686406 | bytes 3392847 | solution.py:46
  53.8 1.7 fusion.79
  57.8 1.7 fusion.79
  77.5 17.5 %all_gather.21 = f32[2,49152]{1,0:T(2,128)} all-gather(f32[2,6144]{1,0:T(2,128)S(1)} %copy-done.7), channel_id=1, replica_groups=mesh['cls'=4,'org'=8] {'org'}, dimensions={1}, use_global_device_ids=true | all-gather | bytes 442368 | tf_op jit(solution)/shard_map/all_gather | solution.py:87
  95.7 42.7 %all-reduce.4.cloned.1.call-done = (f32[2,49152]{1,0:T(2,128)}, f32[2,49152]{1,0:T(2,128)}) async-done(((f32[2,49152]{1,0:T(2,128)}, f32[2,49152]{1,0:T(2,128)}), (f32[2,49152]{1,0:T(2,128)}, f32[2,49152]{1,0:T(2,128)})) %all-reduce.4.cloned.1.call-update) | async-done | bytes 786448 | tf_op jit(solution)/shard_map/psum | solution.py:99
  138.4 3.8 multiply_add_fusion
  143.5 15.2 %all_gather.25 = f32[49152]{0:T(1024)} all-gather(f32[6144]{0:T(1024)S(1)} %copy-done.9), channel_id=1, replica_groups=mesh['cls'=4,'org'=8] {'org'}, dimensions={0}, use_global_device_ids=true | all-gather | bytes 221184 | tf_op jit(solution)/shard_map/all_gather | solution.py:86
  158.7 14.7 %all_gather.22 = f32[2,49152]{1,0:T(2,128)S(1)} all-gather(f32[2,6144]{1,0:T(2,128)S(1)} %copy-done.8), channel_id=1, replica_groups=mesh['cls'=4,'org'=8] {'org'}, dimensions={1}, use_global_device_ids=true | all-gather | bytes 442368 | tf_op jit(solution)/shard_map/all_gather | solution.py:85
  174.8 2.5 reshape.94
  177.3 2.5 reshape.92
  179.8 24.8 %all-gather.14.cloned.1.call-done = f32[4,2,49152]{2,1,0:T(2,128)} async-done(((f32[1,2,49152]{2,1,0:T(2,128)}), f32[4,2,49152]{2,1,0:T(2,128)}) %all-gather.14.cloned.1.call-update) | async-done | bytes 1572880 | tf_op jit(solution)/shard_map/all_gather | solution.py:91
  204.6 3.6 reshape.96
  208.2 36.0 %all-gather.8.cloned.1.call-done = f32[2,8,49152]{2,1,0:T(8,128)} async-done(((f32[2,8,6144]{2,1,0:T(8,128)}), f32[2,8,49152]{2,1,0:T(8,128)}) %all-gather.8.cloned.1.call-update) | async-done | bytes 3145744 | tf_op jit(solution)/shard_map/all_gather | solution.py:84
  244.2 6.9 %multiply_reduce_fusion.1 = (f32[49152,2]{0,1:T(2,128)S(1)}, f32[49152,2]{0,1:T(2,128)S(1)}, f32[49152,2]{0,1:T(2,128)}) fusion(f32[2,8,49152]{2,1,0:T(8,128)} %all-gather.8.cloned.1.call-done, f32[49152,8]{0,1:T(8,128)S(1)} %bitcast.155, f32[49152,8]{0,1:T(8,128)} %bitcast.157, f32[49152,8]{0,1:T(8,128)S(1)} %bitcast.156), kind=kLoop, calls=%fused_computation.59 | loop fusion | flops 4423680 | bytes 9043968 | tf_op jit(solution)/shard_map/cel,el->cl/dot_general | solution.py:19
  253.4 39.4 %while.44 = (s32[]{:T(128)}, f32[2,1,60]{2,0,1:T(2,128)S(1)}, s32[8]{0:T(128)S(1)}, f32[2,49152]{1,0:T(2,128)S(1)}, s32[2,1,2,49152]{3,0,2,1:T(2,128)}, /*index=5*/s32[]{:T(128)}, s32[1]{0:T(128)}, s32[]{:T(128)}, s32[]{:T(128)}) while((s32[]{:T(128)}, f32[2,1,60]{2,0,1:T(2,128)S(1)}, s32[8]{0:T(128)S(1)}, ...), condition=%wide.region_8.9_spmd.clone, body=%wide.region_6.8_spmd.clone.sunk | while | flops 6943207 | bytes 3615725 | solution.py:62
  294.2 39.4 %while.45 = (s32[]{:T(128)}, f32[2,1,60]{2,0,1:T(2,128)S(1)}, s32[8]{0:T(128)S(1)}, f32[2,49152]{1,0:T(2,128)S(1)}, s32[2,1,2,49152]{3,0,2,1:T(2,128)}, /*index=5*/s32[]{:T(128)}, s32[1]{0:T(128)}, s32[]{:T(128)}, s32[]{:T(128)}) while((s32[]{:T(128)}, f32[2,1,60]{2,0,1:T(2,128)S(1)}, s32[8]{0:T(128)S(1)}, ...), condition=%wide.region_11.12_spmd.clone, body=%wide.region_9.11_spmd.clone.sunk | while | flops 6943207 | bytes 3615725 | solution.py:62
  334.2 39.7 %all-reduce = (f32[]{:T(128)}, f32[]{:T(128)}, f32[]{:T(128)}, f32[]{:T(128)}) all-reduce(f32[]{:T(128)} %fusion.53, f32[]{:T(128)} %get-tuple-element.186, f32[]{:T(128)} %fusion.54, f32[]{:T(128)} %get-tuple-element.185), channel_id=1, replica_groups=mesh['cls'=4,'org'=8] {'cls','org'}, use_global_device_ids=true, to_apply=%region_17.18 | all-reduce | flops 4 | bytes 32 | tf_op jit(solution)/shard_map/psum | solution.py:69
  (353 shorter events, 121.2 us)
Async XLA Ops:
  8.0 130.4 %all-reduce.4.cloned.1.call-start = ((), (), s32[]{:S(2)}) async-start(), calls=%async_computation.4 | async-start | bytes 1572864 | tf_op jit(solution)/shard_map/psum | solution.py:99
  8.0 1.5 copy-start.11
  43.2 1.0 copy-start
  43.2 1.1 copy-start.6
  43.3 34.1 %copy-start.7 = (f32[2,6144]{1,0:T(2,128)S(1)}, f32[2,6144]{1,0:T(2,128)}, u32[]{:S(2)}) copy-start(f32[2,6144]{1,0:T(2,128)} %param.15) | copy-start | bytes 147460
  76.6 0.8 copy-start.5
  76.6 65.5 %copy-start.1 = (s32[2,1,2,49152]{3,0,2,1:T(2,128)}, s32[2,1,2,49152]{3,0,2,1:T(2,128)S(1)}, u32[]{:S(2)}) copy-start(s32[2,1,2,49152]{3,0,2,1:T(2,128)S(1)} %get-tuple-element.496) | copy-start | bytes 2359300
  76.6 18.4 %copy-start.10 = (f32[2]{0:T(128)S(1)}, f32[2]{0:T(128)}, u32[]{:S(2)}) copy-start(f32[2]{0:T(128)} %param.21) | copy-start | bytes 28
  77.4 97.4 %all-gather.12.cloned.1.call-start = ((), (), s32[]{:S(2)}) async-start(), calls=%async_computation.2 | async-start | bytes 1966080 | tf_op jit(solution)/shard_map/all_gather | solution.py:91
  95.0 82.3 %all-gather.10.cloned.1.call-start = ((), (), s32[]{:S(2)}) async-start(), calls=%async_computation.1 | async-start | bytes 1966080 | tf_op jit(solution)/shard_map/all_gather | solution.py:91
  138.4 5.1 %copy-start.9 = (f32[6144]{0:T(1024)S(1)}, f32[6144]{0:T(1024)}, u32[]{:S(2)}) copy-start(f32[6144]{0:T(1024)} %param.18) | copy-start | bytes 73732
  138.4 20.3 %copy-start.8 = (f32[2,6144]{1,0:T(2,128)S(1)}, f32[2,6144]{1,0:T(2,128)}, u32[]{:S(2)}) copy-start(f32[2,6144]{1,0:T(2,128)} %param.17) | copy-start | bytes 147460
  142.2 62.4 %all-gather.14.cloned.1.call-start = ((), (), s32[]{:S(2)}) async-start(), calls=%async_computation.3 | async-start | bytes 1966080 | tf_op jit(solution)/shard_map/all_gather | solution.py:91
  142.8 101.5 %all-gather.8.cloned.1.call-start = ((), (), s32[]{:S(2)}) async-start(), calls=%async_computation | async-start | bytes 3538944 | tf_op jit(solution)/shard_map/all_gather | solution.py:84
  244.2 6.9 %copy-start.2 = (f32[49152]{0:T(1024)S(1)}, f32[49152]{0:T(1024)}, u32[]{:S(2)}) copy-start(f32[49152]{0:T(1024)} %all_gather.25) | copy-start | bytes 589828
  294.2 83.5 %copy-start.3 = (f32[49152]{0:T(1024)S(1)}, f32[49152]{0:T(1024)}, u32[]{:S(2)}) copy-start(f32[49152]{0:T(1024)} %all_gather.25) | copy-start | bytes 589828
  294.2 83.5 %copy-start.4 = (f32[49152,2]{0,1:T(2,128)S(1)}, f32[49152,2]{0,1:T(2,128)}, u32[]{:S(2)}) copy-start(f32[49152,2]{0,1:T(2,128)} %get-tuple-element.184) | copy-start | bytes 1179652
Sparse Core Ops, SparseCore 0:
  77.5 60.7 all-reduce.3
Sparse Core Ops, SparseCore 1:
  95.1 31.7 all-gather.11
  142.3 29.8 all-gather.9
  173.8 30.7 all-gather.13
  206.2 38.0 all-gather.7
where the time goes:
time: 389 us; the launch traced here: 387 us
  waiting for transfers between devices  105 us (27%)
  blocking collectives  87 us (22%)
  other arithmetic  73.1 us (19%)
  local copies, waits for them, and re-layouts  54.4 us (14%)
  matrix products  25.3 us (7%)
  loops' own time  22.7 us (6%)
  between operations  19.7 us (5%)
    convert_element_type x32, other arithmetic, unpack_half(): return bit_table.reshape(new_shape).astype(jnp.bfloat16)  55.2 us
    psum x1, waiting for transfers between devices, shards(): aon = lax.psum(partial_value, 'org')  42.7 us
    psum x1, blocking collectives, both_totals(): return lax.psum((cost_part, path_part), ('cls', 'org'))  39.7 us
    all_gather x1, waiting for transfers between devices, shards(): lax.all_gather(interaction, 'org', axis=2, tiled=True)  36 us
    all_gather x3, waiting for transfers between devices, full_cost(): flows_all = lax.all_gather(flow_value, 'cls', axis=0, tiled=True)  24.8 us
    dynamic_slice x32, local copies, waits for them, and re-layouts, fold_links(): lax.scan(advance, skim_carry, jnp.arange(turn_count, dtype=jnp.int32))  18.8 us
    all_gather x1, blocking collectives, shards(): lax.all_gather(flows_start, 'org', axis=1, tiled=True)  17.5 us
    shift_right_arithmetic x96, local copies, waits for them, and re-layouts, unpack_half(): jnp.right_shift(packed[..., :, None, :], shifts[:, None])  17.5 us
  transfers between devices with their start and end apart: 5, of which 3 were waited for; matrix products, arithmetic and copies ran while one was open for 4% of the time, Pallas kernels for 0%

commit v1 on v0

--- a/solution.py
+++ b/solution.py
@@ -88,7 +88,14 @@
     )
 
     def full_cost(flow_value):
-        flows_all = lax.all_gather(flow_value, "cls", axis=0, tiled=True)
+        ring = [flow_value]
+        for hop in range(3):
+            ring.append(lax.ppermute(ring[-1], "cls", [(dev, (dev + 1) % 4) for dev in range(4)]))
+        flows_all = jnp.roll(
+            jnp.concatenate(ring[::-1], axis=0),
+            (lax.axis_index("cls") + 1) * ring[0].shape[0],
+            axis=0,
+        )
         return link_cost(flows_all, inter_full, free_full, cap_full)
 
     for iteration in range(ITERS):

time: 389 us -> 371 us (0.954)
  waiting for transfers between devices: 105 us -> 76.5 us
  other arithmetic: 73.1 us -> 85 us
  local copies, waits for them, and re-layouts: 54.4 us -> 44.9 us
  starting transfers between devices: 0.21 us -> 9.25 us
    all_gather x1, waiting for transfers between devices: 36 us -> 0.01 us  [shards(): lax.all_gather(interaction, 'org', axis=2, tiled=True)]
    ppermute x0 -> x9, waiting for transfers between devices: none -> 34.3 us  [full_cost(): lax.ppermute(ring[-1], 'cls', [(dev, (dev + 1) % 4) for dev in range(4)])]
    all_gather x3 -> x0, waiting for transfers between devices: 24.8 us -> none  [full_cost(): flows_all = lax.all_gather(flow_value, 'cls', axis=0, tiled=True)]
    unnamed x2 -> x5, other arithmetic: 0.01 us -> 12.9 us
    ppermute x0 -> x9, starting transfers between devices: none -> 9.17 us  [full_cost(): lax.ppermute(ring[-1], 'cls', [(dev, (dev + 1) % 4) for dev in range(4)])]
    unnamed x27 -> x42, local copies, waits for them, and re-layouts: 10.4 us -> 1.65 us
  transfers between devices with their start and end apart: 5 -> 11, of which waited for: 3 -> 6; matrix products, arithmetic and copies ran while one was open for 4% -> 5% of each run, Pallas kernels for 0% -> 0%
where the time goes in v1:
time: 371 us; the launch traced here: 370 us
  blocking collectives  88 us (24%)
  other arithmetic  85 us (23%)
  waiting for transfers between devices  76.5 us (21%)
  local copies, waits for them, and re-layouts  44.9 us (12%)
  matrix products  25.3 us (7%)
  loops' own time  22.7 us (6%)
  between operations  18.4 us (5%)
  starting transfers between devices  9.25 us (2%)
    convert_element_type x32, other arithmetic, unpack_half(): return bit_table.reshape(new_shape).astype(jnp.bfloat16)  55.2 us
    psum x1, waiting for transfers between devices, shards(): aon = lax.psum(partial_value, 'org')  42.1 us
    psum x1, blocking collectives, both_totals(): return lax.psum((cost_part, path_part), ('cls', 'org'))  38 us
    ppermute x9, waiting for transfers between devices, full_cost(): lax.ppermute(ring[-1], 'cls', [(dev, (dev + 1) % 4) for dev in range(4)])  34.3 us
    dynamic_slice x32, local copies, waits for them, and re-layouts, fold_links(): lax.scan(advance, skim_carry, jnp.arange(turn_count, dtype=jnp.int32))  18.8 us
    shift_right_arithmetic x96, local copies, waits for them, and re-layouts, unpack_half(): jnp.right_shift(packed[..., :, None, :], shifts[:, None])  17.5 us
    all_gather x1, blocking collectives, shards(): lax.all_gather(free_time, 'org', axis=1, tiled=True)  17.4 us
    all_gather x1, blocking collectives, shards(): lax.all_gather(flows_start, 'org', axis=1, tiled=True)  16.7 us
  transfers between devices with their start and end apart: 11, of which 6 were waited for; matrix products, arithmetic and copies ran while one was open for 5% of the time, Pallas kernels for 0%

profile of v1, /device:TPU:0, one launch (start us, length us, event | category | flops | bytes accessed | tf_op | source)
XLA Modules:
  0.0 370.1 jit_solution(3126476462378488224)
XLA Ops:
  10.1 32.3 %while.43 = (s32[]{:T(128)}, f32[8,2,6144]{2,1,0:T(2,128)S(1)}, s32[8]{0:T(128)S(1)}, s32[2,1,2,49152]{3,0,2,1:T(2,128)S(1)}, bf16[2,1,60]{2,0,1:T(2,128)(2,1)S(...) while((s32[]{:T(128)}, f32[8,2,6144]{2,1,0:T(2,128)S(1)}, s32[8]{0:T(128)S(1)}, ...), condition=%wide.region_4.5_spmd, body=%wide.region_3.4_spmd.sunk | while | flops 3686406 | bytes 3392847 | solution.py:46
  11.4 1.7 fusion.107
  15.5 1.7 fusion.107
  19.5 1.7 fusion.107
  23.5 1.7 fusion.107
  27.6 1.7 fusion.107
  43.4 32.3 %while.42 = (s32[]{:T(128)}, f32[8,2,6144]{2,1,0:T(2,128)S(1)}, s32[8]{0:T(128)S(1)}, s32[2,1,2,49152]{3,0,2,1:T(2,128)S(1)}, bf16[2,1,60]{2,0,1:T(2,128)(2,1)S(...) while((s32[]{:T(128)}, f32[8,2,6144]{2,1,0:T(2,128)S(1)}, s32[8]{0:T(128)S(1)}, ...), condition=%wide.region_1.2_spmd, body=%wide.region_0.1_spmd.sunk | while | flops 3686406 | bytes 3392847 | solution.py:46
  76.5 16.7 %all_gather.12 = f32[2,49152]{1,0:T(2,128)S(1)} all-gather(f32[2,6144]{1,0:T(2,128)S(1)} %copy-done.16), channel_id=1, replica_groups=mesh['cls'=4,'org'=8] {'org'}, dimensions={1}, use_global_device_ids=true | all-gather | bytes 442368 | tf_op jit(solution)/shard_map/all_gather | solution.py:87
  95.2 42.1 %all-reduce.4.cloned.1.call-done = (f32[2,49152]{1,0:T(2,128)}, f32[2,49152]{1,0:T(2,128)}) async-done(((f32[2,49152]{1,0:T(2,128)}, f32[2,49152]{1,0:T(2,128)}), (f32[2,49152]{1,0:T(2,128)}, f32[2,49152]{1,0:T(2,128)})) %all-reduce.4.cloned.1.call-update) | async-done | bytes 786448 | tf_op jit(solution)/shard_map/psum | solution.py:106
  137.3 2.7 multiply_add_fusion
  144.6 16.0 %all_gather.15 = f32[49152]{0:T(1024)} all-gather(f32[6144]{0:T(1024)S(1)} %copy-done.18), channel_id=1, replica_groups=mesh['cls'=4,'org'=8] {'org'}, dimensions={0}, use_global_device_ids=true | all-gather | bytes 221184 | tf_op jit(solution)/shard_map/all_gather | solution.py:86
  160.6 17.4 %all_gather.13 = f32[2,49152]{1,0:T(2,128)} all-gather(f32[2,6144]{1,0:T(2,128)S(1)} %copy-done.17), channel_id=1, replica_groups=mesh['cls'=4,'org'=8] {'org'}, dimensions={1}, use_global_device_ids=true | all-gather | bytes 442368 | tf_op jit(solution)/shard_map/all_gather | solution.py:85
  181.9 9.0 %collective-permute-done.1 = f32[2,49152]{1,0:T(2,128)S(1)} collective-permute-done((f32[2,49152]{1,0:T(2,128)S(1)}, f32[2,49152]{1,0:T(2,128)S(1)}, u32[]{:S(2)}, u32[]{:S(2)}) %collective-permute-start.1) | collective-permute-done | bytes 393248 | tf_op jit(solution)/shard_map/ppermute | solution.py:93
  190.8 8.4 %collective-permute-done.7 = f32[2,49152]{1,0:T(2,128)S(1)} collective-permute-done((f32[2,49152]{1,0:T(2,128)S(1)}, f32[2,49152]{1,0:T(2,128)S(1)}, u32[]{:S(2)}, u32[]{:S(2)}) %collective-permute-start.7) | collective-permute-done | bytes 393248 | tf_op jit(solution)/shard_map/ppermute | solution.py:93
  199.3 8.4 %collective-permute-done.5 = f32[2,49152]{1,0:T(2,128)S(1)} collective-permute-done((f32[2,49152]{1,0:T(2,128)S(1)}, f32[2,49152]{1,0:T(2,128)S(1)}, u32[]{:S(2)}, u32[]{:S(2)}) %collective-permute-start.5) | collective-permute-done | bytes 393248 | tf_op jit(solution)/shard_map/ppermute | solution.py:93
  207.7 3.9 %fusion.56 = f32[49152,8]{0,1:T(8,128)S(1)} fusion(s32[]{:T(128)S(6)} %select_n.38, f32[2,49152]{1,0:T(2,128)S(1)} %collective-permute-done.5, f32[2,49152]{1,0:T(2,128)S(1)} %collective-permute-done.4, f32[2,49152]{1,0:T(2,128)S(1)} %collective-permute-done.3, f32[2,49152]{1,0:T(2,128)S(1)} %all_gather.12), kind=kLoop, calls=%fused_computation.97 | loop fusion | flops 2752512 | bytes 3145732
  211.6 4.5 %collective-permute-done.2 = f32[2,49152]{1,0:T(2,128)S(1)} collective-permute-done((f32[2,49152]{1,0:T(2,128)S(1)}, f32[2,49152]{1,0:T(2,128)S(1)}, u32[]{:S(2)}, u32[]{:S(2)}) %collective-permute-start.2) | collective-permute-done | bytes 393248 | tf_op jit(solution)/shard_map/ppermute | solution.py:93
  216.1 3.9 %fusion.64 = f32[49152,8]{0,1:T(8,128)S(1)} fusion(s32[]{:T(128)S(6)} %select_n.38, f32[2,49152]{1,0:T(2,128)S(1)} %collective-permute-done.2, f32[2,49152]{1,0:T(2,128)S(1)} %collective-permute-done.1, f32[2,49152]{1,0:T(2,128)S(1)} %copy-done.15, f32[2,49152]{1,0:T(2,128)S(1)} %copy-done.5), kind=kLoop, calls=%fused_computation.105 | loop fusion | flops 2752512 | bytes 3145732
  220.0 4.0 %collective-permute-done.8 = f32[2,49152]{1,0:T(2,128)S(1)} collective-permute-done((f32[2,49152]{1,0:T(2,128)S(1)}, f32[2,49152]{1,0:T(2,128)S(1)}, u32[]{:S(2)}, u32[]{:S(2)}) %collective-permute-start.8) | collective-permute-done | bytes 393248 | tf_op jit(solution)/shard_map/ppermute | solution.py:93
  224.0 5.2 %fusion.48 = f32[49152,8]{0,1:T(8,128)} fusion(s32[]{:T(128)S(6)} %select_n.38, f32[2,49152]{1,0:T(2,128)S(1)} %collective-permute-done.8, f32[2,49152]{1,0:T(2,128)S(1)} %collective-permute-done.7, f32[2,49152]{1,0:T(2,128)S(1)} %copy-done.13, f32[2,49152]{1,0:T(2,128)S(1)} %copy-done.3), kind=kLoop, calls=%fused_computation.89 | loop fusion | flops 2752512 | bytes 3145732
  229.2 6.9 %multiply_reduce_fusion.1 = (f32[49152,2]{0,1:T(2,128)S(1)}, f32[49152,2]{0,1:T(2,128)S(1)}, f32[49152,2]{0,1:T(2,128)}) fusion(f32[2,8,49152]{2,1,0:T(8,128)} %all-gather.2.cloned.1.call-done, f32[49152,8]{0,1:T(8,128)S(1)} %fusion.56, f32[49152,8]{0,1:T(8,128)} %fusion.48, f32[49152,8]{0,1:T(8,128)S(1)} %fusion.64), kind=kLoop, calls=%fused_computation.83 | loop fusion | flops 4423680 | bytes 9043968 | tf_op jit(solution)/shard_map/cel,el->cl/dot_general | solution.py:19
  237.6 39.4 %while.44 = (s32[]{:T(128)}, f32[2,1,60]{2,0,1:T(2,128)S(1)}, s32[8]{0:T(128)S(1)}, f32[2,49152]{1,0:T(2,128)S(1)}, s32[2,1,2,49152]{3,0,2,1:T(2,128)}, /*index=5*/s32[]{:T(128)}, s32[1]{0:T(128)}, s32[]{:T(128)}, s32[]{:T(128)}) while((s32[]{:T(128)}, f32[2,1,60]{2,0,1:T(2,128)S(1)}, s32[8]{0:T(128)S(1)}, ...), condition=%wide.region_8.10_spmd.clone, body=%wide.region_6.9_spmd.clone.sunk | while | flops 6943207 | bytes 3615725 | solution.py:62
  278.4 39.4 %while.45 = (s32[]{:T(128)}, f32[2,1,60]{2,0,1:T(2,128)S(1)}, s32[8]{0:T(128)S(1)}, f32[2,49152]{1,0:T(2,128)S(1)}, s32[2,1,2,49152]{3,0,2,1:T(2,128)}, /*index=5*/s32[]{:T(128)}, s32[1]{0:T(128)}, s32[]{:T(128)}, s32[]{:T(128)}) while((s32[]{:T(128)}, f32[2,1,60]{2,0,1:T(2,128)S(1)}, s32[8]{0:T(128)S(1)}, ...), condition=%wide.region_11.13_spmd.clone, body=%wide.region_9.12_spmd.clone.sunk | while | flops 6943207 | bytes 3615725 | solution.py:62
  318.4 38.0 %all-reduce = (f32[]{:T(128)}, f32[]{:T(128)}, f32[]{:T(128)}, f32[]{:T(128)}) all-reduce(f32[]{:T(128)} %fusion.77, f32[]{:T(128)} %get-tuple-element.187, f32[]{:T(128)} %fusion.78, f32[]{:T(128)} %get-tuple-element.186), channel_id=1, replica_groups=mesh['cls'=4,'org'=8] {'cls','org'}, use_global_device_ids=true, to_apply=%region_17.19 | all-reduce | flops 4 | bytes 32 | tf_op jit(solution)/shard_map/psum | solution.py:69
  (380 shorter events, 133.4 us)
Async XLA Ops:
  7.2 130.1 %all-reduce.4.cloned.1.call-start = ((), (), s32[]{:S(2)}) async-start(), calls=%async_computation.1 | async-start | bytes 1572864 | tf_op jit(solution)/shard_map/psum | solution.py:106
  42.5 34.0 %copy-start.16 = (f32[2,6144]{1,0:T(2,128)S(1)}, f32[2,6144]{1,0:T(2,128)}, u32[]{:S(2)}) copy-start(f32[2,6144]{1,0:T(2,128)} %param.17) | copy-start | bytes 147460
  42.5 52.1 %copy-start.19 = (f32[2]{0:T(128)S(1)}, f32[2]{0:T(128)}, u32[]{:S(2)}) copy-start(f32[2]{0:T(128)} %param.23) | copy-start | bytes 28
  75.7 64.4 %copy-start.1 = (s32[2,1,2,49152]{3,0,2,1:T(2,128)}, s32[2,1,2,49152]{3,0,2,1:T(2,128)S(1)}, u32[]{:S(2)}) copy-start(s32[2,1,2,49152]{3,0,2,1:T(2,128)S(1)} %get-tuple-element.494) | copy-start | bytes 2359300
  76.4 68.2 %copy-start.18 = (f32[6144]{0:T(1024)S(1)}, f32[6144]{0:T(1024)}, u32[]{:S(2)}) copy-start(f32[6144]{0:T(1024)} %param.20) | copy-start | bytes 73732
  76.4 84.2 %copy-start.17 = (f32[2,6144]{1,0:T(2,128)S(1)}, f32[2,6144]{1,0:T(2,128)}, u32[]{:S(2)}) copy-start(f32[2,6144]{1,0:T(2,128)} %param.19) | copy-start | bytes 147460
  76.5 152.7 %all-gather.2.cloned.1.call-start = ((), (), s32[]{:S(2)}) async-start(), calls=%async_computation | async-start | bytes 3538944 | tf_op jit(solution)/shard_map/all_gather | solution.py:84
  93.2 49.9 %collective-permute-start.3 = (f32[2,49152]{1,0:T(2,128)S(1)}, f32[2,49152]{1,0:T(2,128)S(1)}, u32[]{:S(2)}, u32[]{:S(2)}) collective-permute-start(f32[2,49152]{1,0:T(2,128)S(1)} %all_gather.12), channel_id=1, source_target_pairs={{0,8},{8,16},{16,24},{24,0},{1,9},{9,17},{17,25},{25,1},{2,10},{10... | collective-permute-start | bytes 1179656 | tf_op jit(solution)/shard_map/ppermute | solution.py:93
  140.1 59.2 %copy-start.2 = (f32[2,49152]{1,0:T(2,128)}, f32[2,49152]{1,0:T(2,128)S(1)}, u32[]{:S(2)}) copy-start(f32[2,49152]{1,0:T(2,128)S(1)} %get-tuple-element.235) | copy-start | bytes 1179652
  140.1 59.2 %copy-start.4 = (f32[2,49152]{1,0:T(2,128)}, f32[2,49152]{1,0:T(2,128)S(1)}, u32[]{:S(2)}) copy-start(f32[2,49152]{1,0:T(2,128)S(1)} %get-tuple-element.234) | copy-start | bytes 1179652
  140.1 37.9 %collective-permute-start = (f32[2,49152]{1,0:T(2,128)S(1)}, f32[2,49152]{1,0:T(2,128)S(1)}, u32[]{:S(2)}, u32[]{:S(2)}) collective-permute-start(f32[2,49152]{1,0:T(2,128)S(1)} %get-tuple-element.234), channel_id=1, source_target_pairs={{0,8},{8,16},{16,24},{24,0},{1,9},{9,17},{17,25},{25,1},{2,10},{10... | collective-permute-start | bytes 1179656 | tf_op jit(solution)/shard_map/ppermute | solution.py:93
  141.6 36.7 %collective-permute-start.6 = (f32[2,49152]{1,0:T(2,128)S(1)}, f32[2,49152]{1,0:T(2,128)S(1)}, u32[]{:S(2)}, u32[]{:S(2)}) collective-permute-start(f32[2,49152]{1,0:T(2,128)S(1)} %get-tuple-element.235), channel_id=1, source_target_pairs={{0,8},{8,16},{16,24},{24,0},{1,9},{9,17},{17,25},{25,1},{2,10},{10... | collective-permute-start | bytes 1179656 | tf_op jit(solution)/shard_map/ppermute | solution.py:93
  143.1 36.7 %collective-permute-start.4 = (f32[2,49152]{1,0:T(2,128)S(1)}, f32[2,49152]{1,0:T(2,128)S(1)}, u32[]{:S(2)}, u32[]{:S(2)}) collective-permute-start(f32[2,49152]{1,0:T(2,128)S(1)} %collective-permute-done.3), channel_id=1, source_target_pairs={{0,8},{8,16},{16,24},{24,0},{1,9},{9,17},{17,25},{25,1},{2,10},{10... | collective-permute-start | bytes 1179656 | tf_op jit(solution)/shard_map/ppermute | solution.py:93
  178.0 21.3 %copy-start.14 = (f32[2,49152]{1,0:T(2,128)}, f32[2,49152]{1,0:T(2,128)S(1)}, u32[]{:S(2)}) copy-start(f32[2,49152]{1,0:T(2,128)S(1)} %collective-permute-done) | copy-start | bytes 1179652
  178.0 12.9 %collective-permute-start.1 = (f32[2,49152]{1,0:T(2,128)S(1)}, f32[2,49152]{1,0:T(2,128)S(1)}, u32[]{:S(2)}, u32[]{:S(2)}) collective-permute-start(f32[2,49152]{1,0:T(2,128)S(1)} %collective-permute-done), channel_id=1, source_target_pairs={{0,8},{8,16},{16,24},{24,0},{1,9},{9,17},{17,25},{25,1},{2,10},{10... | collective-permute-start | bytes 1179656 | tf_op jit(solution)/shard_map/ppermute | solution.py:93
  178.3 21.0 %copy-start.12 = (f32[2,49152]{1,0:T(2,128)}, f32[2,49152]{1,0:T(2,128)S(1)}, u32[]{:S(2)}) copy-start(f32[2,49152]{1,0:T(2,128)S(1)} %collective-permute-done.6) | copy-start | bytes 1179652
  178.3 21.0 %collective-permute-start.7 = (f32[2,49152]{1,0:T(2,128)S(1)}, f32[2,49152]{1,0:T(2,128)S(1)}, u32[]{:S(2)}, u32[]{:S(2)}) collective-permute-start(f32[2,49152]{1,0:T(2,128)S(1)} %collective-permute-done.6), channel_id=1, source_target_pairs={{0,8},{8,16},{16,24},{24,0},{1,9},{9,17},{17,25},{25,1},{2,10},{10... | collective-permute-start | bytes 1179656 | tf_op jit(solution)/shard_map/ppermute | solution.py:93
  179.8 27.9 %collective-permute-start.5 = (f32[2,49152]{1,0:T(2,128)S(1)}, f32[2,49152]{1,0:T(2,128)S(1)}, u32[]{:S(2)}, u32[]{:S(2)}) collective-permute-start(f32[2,49152]{1,0:T(2,128)S(1)} %collective-permute-done.4), channel_id=1, source_target_pairs={{0,8},{8,16},{16,24},{24,0},{1,9},{9,17},{17,25},{25,1},{2,10},{10... | collective-permute-start | bytes 1179656 | tf_op jit(solution)/shard_map/ppermute | solution.py:93
  190.8 25.3 %collective-permute-start.2 = (f32[2,49152]{1,0:T(2,128)S(1)}, f32[2,49152]{1,0:T(2,128)S(1)}, u32[]{:S(2)}, u32[]{:S(2)}) collective-permute-start(f32[2,49152]{1,0:T(2,128)S(1)} %collective-permute-done.1), channel_id=1, source_target_pairs={{0,8},{8,16},{16,24},{24,0},{1,9},{9,17},{17,25},{25,1},{2,10},{10... | collective-permute-start | bytes 1179656 | tf_op jit(solution)/shard_map/ppermute | solution.py:93
  199.3 24.7 %collective-permute-start.8 = (f32[2,49152]{1,0:T(2,128)S(1)}, f32[2,49152]{1,0:T(2,128)S(1)}, u32[]{:S(2)}, u32[]{:S(2)}) collective-permute-start(f32[2,49152]{1,0:T(2,128)S(1)} %collective-permute-done.7), channel_id=1, source_target_pairs={{0,8},{8,16},{16,24},{24,0},{1,9},{9,17},{17,25},{25,1},{2,10},{10... | collective-permute-start | bytes 1179656 | tf_op jit(solution)/shard_map/ppermute | solution.py:93
  211.6 12.4 %copy-start.3 = (f32[2,49152]{1,0:T(2,128)S(1)}, f32[2,49152]{1,0:T(2,128)}, u32[]{:S(2)}) copy-start(f32[2,49152]{1,0:T(2,128)} %copy-done.2) | copy-start | bytes 1179652
  211.6 12.4 %copy-start.13 = (f32[2,49152]{1,0:T(2,128)S(1)}, f32[2,49152]{1,0:T(2,128)}, u32[]{:S(2)}) copy-start(f32[2,49152]{1,0:T(2,128)} %copy-done.12) | copy-start | bytes 1179652
  278.4 82.0 %copy-start.8 = (f32[49152]{0:T(1024)S(1)}, f32[49152]{0:T(1024)}, u32[]{:S(2)}) copy-start(f32[49152]{0:T(1024)} %all_gather.15) | copy-start | bytes 589828
  278.4 82.0 %copy-start.9 = (f32[49152,2]{0,1:T(2,128)S(1)}, f32[49152,2]{0,1:T(2,128)}, u32[]{:S(2)}) copy-start(f32[49152,2]{0,1:T(2,128)} %get-tuple-element.185) | copy-start | bytes 1179652
  (8 other events, 34.8 us)
Sparse Core Ops, SparseCore 0:
  76.5 60.7 all-reduce.3
  144.7 39.9 all-gather.1
